TPU v7x, 32 devices: a whole 2x2x4 slice. The times are simulated.
32 devices in a mesh: section: 2 (over core), dp: 8 (over z, x), tensor: 2 (over y).
Axes of the slice: x: 2, y: 2, z: 4, core: 2. Of those that a mesh axis runs over, the one named last changes fastest.
Arguments:
- tokens: bfloat16 [1024, 4096], P('dp', 'tensor'), may hold values from -6 to 6
- gain: bfloat16 [2, 4096], P('section', 'tensor'), may hold values from 0.099609375 to 1.8984375
- w_up: bfloat16 [2, 4096, 5120], P('section', 'dp', 'tensor'), may hold values from -0.09375 to 0.09375
- w_down: bfloat16 [2, 5120, 4096], P('section', 'tensor', 'dp'), may hold values from -0.078125 to 0.078125
- cotangent: bfloat16 [2, 1024, 4096], P('section', 'dp'), may hold values from -6 to 6
Outputs:
- states: bfloat16 [2, 1024, 4096], P('section', 'dp', 'tensor')
- grad_down: bfloat16 [2, 5120, 4096], P('section', 'tensor', 'dp')
All inputs are finite; a program needn't handle non-finite values.
Results may differ from a plain program's by a relative error of at most 0.02.
Values may be sent and summed in bfloat16 or wider, within the bound.
A program may use at most 128 MiB of HBM per device.

v0:
```python
import jax
import jax.numpy as jnp
from jax import lax
from jax.sharding import PartitionSpec as P

EPS = 1e-06
F32 = jnp.float32
BF16 = jnp.bfloat16


def body(tokens, gain, w_up, w_down, cotangent):
    core = lax.axis_index("section")
    layers = lax.axis_size("section")
    assert layers == 2
    dp_id = lax.axis_index("dp")
    dp_count = lax.axis_size("dp")
    tensor_id = lax.axis_index("tensor")
    tensor_count = lax.axis_size("tensor")
    rows, own_width = tokens.shape
    width = own_width * tensor_count
    slice_width = width // dp_count
    hidden_width = w_up.shape[2]
    half = hidden_width // layers
    other = 1 - core
    all_rows = rows * dp_count

    def swap(array):
        return lax.ppermute(array, "section", [(0, 1), (1, 0)])

    def both(own, got):
        return (jnp.where(core == 0, own, got), jnp.where(core == 0, got, own))

    cot_mine = lax.all_to_all(cotangent[0], "dp", split_axis=1, concat_axis=0, tiled=True)
    half_rows = rows // layers
    tok_half = lax.dynamic_slice_in_dim(tokens, core * half_rows, half_rows, 0)
    tok_full = lax.all_gather(tok_half, "tensor", axis=1, tiled=True)
    tok_f = tok_full.astype(F32)
    sums_half = jnp.sum(tok_f * tok_f, axis=1)
    sums_a, sums_b = both(sums_half, swap(sums_half))
    sums = jnp.concatenate([sums_a, sums_b])
    x_half = lax.all_to_all(tok_full, "dp", split_axis=1, concat_axis=0, tiled=True)
    x_a, x_b = both(x_half, swap(x_half))
    x = jnp.concatenate(
        [
            x_a.reshape(dp_count, half_rows, slice_width),
            x_b.reshape(dp_count, half_rows, slice_width),
        ],
        axis=1,
    ).reshape(all_rows, slice_width)
    gain_all = lax.all_gather(gain, "tensor", axis=1, tiled=True)
    gain_own = lax.dynamic_slice_in_dim(gain_all, dp_id * slice_width, slice_width, 1)
    gains = both(gain_own, swap(gain_own))
    up_parts = both(
        lax.dynamic_slice_in_dim(w_up[0], core * half, half, 1),
        swap(lax.dynamic_slice_in_dim(w_up[0], other * half, half, 1)),
    )
    down_parts = both(
        lax.dynamic_slice_in_dim(w_down[0], core * half, half, 0),
        swap(lax.dynamic_slice_in_dim(w_down[0], other * half, half, 0)),
    )
    states = []
    hiddens = []
    for layer in range(layers):
        x_f = x.astype(F32)
        if layer > 0:
            sums = lax.psum_scatter(
                jnp.sum(x_f * x_f, axis=1), "dp", scatter_dimension=0, tiled=True
            )
        scaled = (x_f * gains[layer].astype(F32)).astype(BF16)
        part = jnp.dot(scaled, up_parts[layer], preferred_element_type=F32).astype(BF16)
        pre = lax.psum_scatter(part, "dp", scatter_dimension=0, tiled=True)
        inverse_rms = lax.rsqrt(sums / width + EPS)
        hidden = jax.nn.gelu(pre.astype(F32) * inverse_rms[:, None], approximate=True).astype(BF16)
        hidden_all = lax.all_gather(hidden, "dp", axis=0, tiled=True)
        hiddens.append(hidden_all)
        out = jnp.dot(hidden_all, down_parts[layer], preferred_element_type=F32)
        mid = all_rows // layers
        keep = lax.dynamic_slice_in_dim(out, core * mid, mid, 0)
        give = lax.dynamic_slice_in_dim(out, other * mid, mid, 0).astype(BF16)
        summed = keep + swap(give).astype(F32)
        if tensor_count == 2:
            sent = summed.astype(BF16)
            got = lax.ppermute(sent, "tensor", [(0, 1), (1, 0)])
            summed = sent.astype(F32) + got.astype(F32)
        else:
            summed = lax.psum(summed.astype(BF16), "tensor").astype(F32)
        x_mid = lax.dynamic_slice_in_dim(x_f, core * mid, mid, 0)
        new_mid = (x_mid + summed).astype(BF16)
        new_a, new_b = both(new_mid, swap(new_mid))
        x = jnp.concatenate([new_a, new_b], axis=0)
        states.append(x)
    state_own = jnp.where(core == 0, states[0], states[1])
    state_rows = lax.all_to_all(state_own, "dp", split_axis=0, concat_axis=1, tiled=True)
    state = lax.dynamic_slice_in_dim(state_rows, tensor_id * own_width, own_width, 1)
    hid_keep = jnp.where(core == 0, hiddens[0], hiddens[1])
    hid_got = swap(jnp.where(core == 0, hiddens[1], hiddens[0]))
    hid_parts = both(hid_keep, hid_got)
    hidden_whole = jnp.concatenate(hid_parts, axis=1)
    grad = lax.dot_general(
        hidden_whole, cot_mine, (((0,), (0,)), ((), ())), preferred_element_type=F32
    ).astype(BF16)
    return (state[None], grad[None])


def solution(mesh):
    placed = (
        P("dp", "tensor"),
        P("section", "tensor"),
        P("section", "dp", "tensor"),
        P("section", "tensor", "dp"),
        P("section", "dp", None),
    )
    return jax.shard_map(
        body,
        mesh=mesh,
        in_specs=placed,
        out_specs=(P("section", "dp", "tensor"), P("section", "tensor", "dp")),
        check_vma=False,
    )
```

profile of v0, /device:TPU:0, one launch (start us, length us, event | category | flops | bytes accessed | tf_op | source)
XLA Modules:
  0.0 413.5 jit_solution(5616129061812105178)
XLA Ops:
  8.2 10.0 %all_gather.12 = bf16[64,4096]{1,0:T(8,128)(2,1)S(1)} all-gather(bf16[64,2048]{1,0:T(8,128)(2,1)S(1)} %constant_dynamic-slice_fusion.2), channel_id=1, replica_groups=mesh['section'=2,'dp'=8,'tensor'=2] {'tensor'}, dimensions={1}, use_global_device_ids=true | all-gather | bytes 786432 | tf_op jit(solution)/shard_map/all_gather | solution.py:36
  19.0 6.2 %all-to-all-start = ((bf16[64,8,512]{2,0,1:T(8,128)(2,1)}), bf16[64,8,512]{2,0,1:T(8,128)(2,1)S(1)}, u32[]{:S(2)}, u32[]{:S(2)}) async-start(bf16[64,8,512]{2,0,1:T(8,128)(2,1)} %bitcast.43), calls=%async_computation | async-start | bytes 1048576 | tf_op jit(solution)/shard_map/all_to_all | solution.py:41
  25.3 2.5 dynamic-slice_bitcast_fusion.1
  27.7 11.2 %all-to-all-done = bf16[64,8,512]{2,0,1:T(8,128)(2,1)S(1)} async-done(((bf16[64,8,512]{2,0,1:T(8,128)(2,1)}), bf16[64,8,512]{2,0,1:T(8,128)(2,1)S(1)}, u32[]{:S(2)}, u32[]{:S(2)}) %all-to-all-start) | async-done | bytes 524320 | tf_op jit(solution)/shard_map/all_to_all | solution.py:41
  38.9 4.3 %all_gather.13 = bf16[1,4096]{1,0:T(2,128)(2,1)S(1)} all-gather(bf16[1,2048]{1,0:T(2,128)(2,1)S(1)} %copy-done.12), channel_id=1, replica_groups=mesh['section'=2,'dp'=8,'tensor'=2] {'tensor'}, dimensions={1}, use_global_device_ids=true | all-gather | bytes 12288 | tf_op jit(solution)/shard_map/all_gather | solution.py:50
  46.4 3.1 convolution_convert_fusion.1
  52.2 68.8 %reduce-scatter.3.cloned.1.call-done = bf16[128,1280]{1,0:T(8,128)(2,1)} async-done(((bf16[1024,1280]{1,0:T(8,128)(2,1)}), bf16[128,1280]{1,0:T(8,128)(2,1)}) %reduce-scatter.3.cloned.1.call-update) | async-done | bytes 327696 | tf_op jit(solution)/shard_map/reduce_scatter | solution.py:71
  120.9 2.0 fusion.30
  123.0 2.5 dynamic-slice_bitcast_fusion
  125.5 3.4 collective-permute-done.4
  128.9 48.4 %all-gather.3.cloned.1.call-done = bf16[1024,1280]{1,0:T(8,128)(2,1)} async-done(((bf16[128,1280]{1,0:T(8,128)(2,1)}), bf16[1024,1280]{1,0:T(8,128)(2,1)}) %all-gather.3.cloned.1.call-update) | async-done | bytes 2621456 | tf_op jit(solution)/shard_map/all_gather | solution.py:74
  177.3 3.7 fusion.10
  183.1 2.1 collective-permute-done.5
  188.2 12.5 %collective-permute-done.6 = bf16[512,512]{1,0:T(8,128)(2,1)S(1)} collective-permute-done((bf16[512,512]{1,0:T(8,128)(2,1)S(1)}, bf16[512,512]{1,0:T(8,128)(2,1)S(1)}, u32[]{:S(2)}, u32[]{:S(2)}) %collective-permute-start.6) | collective-permute-done | bytes 524320 | tf_op jit(solution)/shard_map/ppermute | solution.py:83
  201.0 1.9 collective-permute-done.7
  203.0 4.8 %convolution_convert_fusion = bf16[1024,1280]{1,0:T(8,128)(2,1)} fusion(bf16[512,1280]{1,0:T(8,128)(2,1)} %collective-permute-done.2, pred[]{:T(512)S(6)} %eq.2, bf16[1,512,2560]{2,1,0:T(8,128)(2,1)S(1)} %copy-done.11, s32[]{:T(128)S(6)} %select_n.145, f32[512]{0:T(512)S(1)} %bitcast.52, bf16[512,512]{1,0:T(8,128)(2,1)S(1)} %get-tuple-element.7, ...), kind=kOutput, calls=%fused_computation.6 | convolution fusion | flops 1347289088 | bytes 6293509 | tf_op jit(solution)/shard_map/dot_general | solution.py:70
  209.9 19.5 %all-reduce = f32[1024]{0:T(1024)S(1)} all-reduce(f32[1024]{0:T(1024)S(1)} %multiply_reduce_fusion), channel_id=4, replica_groups=mesh['section'=2,'dp'=8,'tensor'=2] {'dp'}, use_global_device_ids=true, to_apply=%region_4.5.clone | all-reduce | flops 1024 | bytes 8192
  229.5 48.0 %reduce-scatter.5.cloned.1.call-done = bf16[128,1280]{1,0:T(8,128)(2,1)} async-done(((bf16[1024,1280]{1,0:T(8,128)(2,1)}), bf16[128,1280]{1,0:T(8,128)(2,1)}) %reduce-scatter.5.cloned.1.call-update) | async-done | bytes 327696 | tf_op jit(solution)/shard_map/reduce_scatter | solution.py:71
  277.5 2.0 fusion.38
  279.5 54.1 %all-gather.5.cloned.1.call-done = bf16[1024,1280]{1,0:T(8,128)(2,1)} async-done(((bf16[128,1280]{1,0:T(8,128)(2,1)}), bf16[1024,1280]{1,0:T(8,128)(2,1)}) %all-gather.5.cloned.1.call-update) | async-done | bytes 2621456 | tf_op jit(solution)/shard_map/all_gather | solution.py:74
  333.7 4.2 %fusion.11 = f32[1024,512]{1,0:T(8,128)S(1)} fusion(bf16[1024,1280]{1,0:T(8,128)(2,1)} %all-gather.5.cloned.1.call-done, bf16[1280,512]{1,0:T(8,128)(2,1)} %collective-permute-done.4, pred[]{:T(512)S(6)} %eq.2, bf16[1,2560,512]{2,1,0:T(8,128)(2,1)} %param.8, s32[]{:T(128)S(6)} %select_n.145), kind=kOutput, calls=%fused_computation.18 | convolution fusion | flops 1342832640 | bytes 7340037 | tf_op jit(solution)/shard_map/dot_general | solution.py:76
  342.4 2.3 copy.18
  344.7 4.2 %all-to-all-start.2 = ((bf16[128,8,512]{0,2,1:T(8,128)(2,1)}), bf16[128,8,512]{0,2,1:T(8,128)(2,1)}, u32[]{:S(2)}, u32[]{:S(2)}) async-start(bf16[128,8,512]{0,2,1:T(8,128)(2,1)} %bitcast.45), calls=%async_computation.4 | async-start | bytes 2097152 | tf_op jit(solution)/shard_map/all_to_all | solution.py:33
  352.4 12.1 %collective-permute-done.9 = bf16[512,512]{1,0:T(8,128)(2,1)S(1)} collective-permute-done((bf16[512,512]{1,0:T(8,128)(2,1)S(1)}, bf16[512,512]{1,0:T(8,128)(2,1)S(1)}, u32[]{:S(2)}, u32[]{:S(2)}) %collective-permute-start.9) | collective-permute-done | bytes 524320 | tf_op jit(solution)/shard_map/ppermute | solution.py:83
  364.8 1.9 collective-permute-done.10
  368.0 2.3 copy.16
  370.3 4.8 %all-to-all-done.2 = bf16[128,8,512]{0,2,1:T(8,128)(2,1)} async-done(((bf16[128,8,512]{0,2,1:T(8,128)(2,1)}), bf16[128,8,512]{0,2,1:T(8,128)(2,1)}, u32[]{:S(2)}, u32[]{:S(2)}) %all-to-all-start.2) | async-done | bytes 1048608 | tf_op jit(solution)/shard_map/all_to_all | solution.py:33
  375.1 4.4 %all-to-all-start.1 = ((bf16[8,128,512]{1,2,0:T(8,128)(2,1)}), bf16[8,128,512]{1,2,0:T(8,128)(2,1)}, u32[]{:S(2)}, u32[]{:S(2)}) async-start(bf16[8,128,512]{1,2,0:T(8,128)(2,1)} %copy.16), calls=%async_computation.3 | async-start | bytes 2097152 | tf_op jit(solution)/shard_map/all_to_all | solution.py:93
  379.6 2.3 copy.19
  381.8 2.3 broadcast_select_fusion.1
  384.1 4.3 %fusion.7 = bf16[1,2560,512]{2,1,0:T(8,128)(2,1)} fusion(bf16[1024,512]{1,0:T(8,128)(2,1)S(1)} %bitcast.50, bf16[1024,1280]{1,0:T(8,128)(2,1)S(1)} %get-tuple-element.3, bf16[1024,1280]{1,0:T(8,128)(2,1)S(1)} %get-tuple-element.2), kind=kOutput, calls=%fused_computation.5 | convolution fusion | flops 2696151040 | bytes 8912896 | tf_op jit(solution)/shard_map/dot_general | solution.py:99
  388.4 16.5 %all-to-all-done.1 = bf16[8,128,512]{1,2,0:T(8,128)(2,1)} async-done(((bf16[8,128,512]{1,2,0:T(8,128)(2,1)}), bf16[8,128,512]{1,2,0:T(8,128)(2,1)}, u32[]{:S(2)}, u32[]{:S(2)}) %all-to-all-start.1) | async-done | bytes 1048608 | tf_op jit(solution)/shard_map/all_to_all | solution.py:93
  (80 shorter events, 26.6 us)
Async XLA Ops:
  7.2 1.0 copy-start
  19.0 19.8 %copy-start.12 = (bf16[1,2048]{1,0:T(2,128)(2,1)S(1)}, bf16[1,2048]{1,0:T(2,128)(2,1)}, u32[]{:S(2)}) copy-start(bf16[1,2048]{1,0:T(2,128)(2,1)} %param.6) | copy-start | bytes 12292
  19.0 19.8 %all-to-all-start = ((bf16[64,8,512]{2,0,1:T(8,128)(2,1)}), bf16[64,8,512]{2,0,1:T(8,128)(2,1)S(1)}, u32[]{:S(2)}, u32[]{:S(2)}) async-start(bf16[64,8,512]{2,0,1:T(8,128)(2,1)} %bitcast.43), calls=%async_computation | async-start | bytes 1048576 | tf_op jit(solution)/shard_map/all_to_all | solution.py:41
  25.2 95.7 %reduce-scatter.3.cloned.1.call-start = ((), (), s32[]{:S(2)}) async-start(), calls=%async_computation.5 | async-start | bytes 2949120 | tf_op jit(solution)/shard_map/reduce_scatter | solution.py:71
  27.7 17.3 %collective-permute-start.2 = (bf16[512,1280]{1,0:T(8,128)(2,1)}, bf16[512,1280]{1,0:T(8,128)(2,1)}, u32[]{:S(2)}, u32[]{:S(2)}) collective-permute-start(bf16[512,1280]{1,0:T(8,128)(2,1)} %dynamic-slice_bitcast_fusion.1), channel_id=1, source_target_pairs={{0,16},{16,0},{1,17},{17,1},{2,18},{18,2},{3,19},{19,3},{4,20},{20... | collective-permute-start | bytes 3932168 | tf_op jit(solution)/shard_map/ppermute | solution.py:28
  38.9 5.6 %collective-permute-start = (bf16[512,512]{1,0:T(8,128)(2,1)S(1)}, bf16[512,512]{1,0:T(8,128)(2,1)S(1)}, u32[]{:S(2)}, u32[]{:S(2)}) collective-permute-start(bf16[512,512]{1,0:T(8,128)(2,1)S(1)} %bitcast.47), channel_id=1, source_target_pairs={{0,16},{16,0},{1,17},{17,1},{2,18},{18,2},{3,19},{19,3},{4,20},{20... | collective-permute-start | bytes 1572872 | tf_op jit(solution)/shard_map/ppermute | solution.py:28
  43.2 1.2 collective-permute-start.1
  44.6 1.7 copy-start.10
  49.5 127.8 %all-gather.3.cloned.1.call-start = ((), (), s32[]{:S(2)}) async-start(), calls=%async_computation.6 | async-start | bytes 2949120 | tf_op jit(solution)/shard_map/all_gather | solution.py:74
  49.7 2.3 collective-permute-start.3
  123.0 154.5 %reduce-scatter.5.cloned.1.call-start = ((), (), s32[]{:S(2)}) async-start(), calls=%async_computation.7 | async-start | bytes 2949120 | tf_op jit(solution)/shard_map/reduce_scatter | solution.py:71
  125.5 3.4 collective-permute-start.4
  180.9 1.3 copy-start.8
  183.1 2.1 collective-permute-start.5
  186.6 16.3 %copy-start.11 = (bf16[1,512,2560]{2,1,0:T(8,128)(2,1)S(1)}, bf16[1,512,2560]{2,1,0:T(8,128)(2,1)}, u32[]{:S(2)}) copy-start(bf16[1,512,2560]{2,1,0:T(8,128)(2,1)} %param.7) | copy-start | bytes 7864324
  186.7 14.0 %collective-permute-start.6 = (bf16[512,512]{1,0:T(8,128)(2,1)S(1)}, bf16[512,512]{1,0:T(8,128)(2,1)S(1)}, u32[]{:S(2)}, u32[]{:S(2)}) collective-permute-start(bf16[512,512]{1,0:T(8,128)(2,1)S(1)} %add_convert_fusion.3), channel_id=1, source_target_pairs={{0,1},{1,0},{2,3},{3,2},{4,5},{5,4},{6,7},{7,6},{8,9},{9,8},{10,11... | collective-permute-start | bytes 1572872 | tf_op jit(solution)/shard_map/ppermute | solution.py:83
  200.9 2.0 collective-permute-start.7
  203.0 6.7 %copy-start.3 = (bf16[512,512]{1,0:T(8,128)(2,1)}, bf16[512,512]{1,0:T(8,128)(2,1)S(1)}, u32[]{:S(2)}) copy-start(bf16[512,512]{1,0:T(8,128)(2,1)S(1)} %get-tuple-element.6) | copy-start | bytes 1572868
  203.0 6.7 %copy-start.5 = (bf16[512,512]{1,0:T(8,128)(2,1)}, bf16[512,512]{1,0:T(8,128)(2,1)S(1)}, u32[]{:S(2)}) copy-start(bf16[512,512]{1,0:T(8,128)(2,1)S(1)} %get-tuple-element.7) | copy-start | bytes 1572868
  207.8 125.9 %all-gather.5.cloned.1.call-start = ((), (), s32[]{:S(2)}) async-start(), calls=%async_computation.8 | async-start | bytes 2949120 | tf_op jit(solution)/shard_map/all_gather | solution.py:74
  333.6 6.4 %copy-start.1 = (bf16[1024,1280]{1,0:T(8,128)(2,1)S(1)}, bf16[1024,1280]{1,0:T(8,128)(2,1)}, u32[]{:S(2)}) copy-start(bf16[1024,1280]{1,0:T(8,128)(2,1)} %all-gather.3.cloned.1.call-done) | copy-start | bytes 7864324
  333.6 6.4 %copy-start.2 = (bf16[1024,1280]{1,0:T(8,128)(2,1)S(1)}, bf16[1024,1280]{1,0:T(8,128)(2,1)}, u32[]{:S(2)}) copy-start(bf16[1024,1280]{1,0:T(8,128)(2,1)} %all-gather.5.cloned.1.call-done) | copy-start | bytes 7864324
  337.8 1.3 copy-start.7
  340.0 8.9 %collective-permute-start.8 = (bf16[512,512]{1,0:T(8,128)(2,1)}, bf16[512,512]{1,0:T(8,128)(2,1)}, u32[]{:S(2)}, u32[]{:S(2)}) collective-permute-start(bf16[512,512]{1,0:T(8,128)(2,1)} %dynamic-slice_convert_fusion), channel_id=1, source_target_pairs={{0,16},{16,0},{1,17},{17,1},{2,18},{18,2},{3,19},{19,3},{4,20},{20... | collective-permute-start | bytes 1572872 | tf_op jit(solution)/shard_map/ppermute | solution.py:28
  341.9 40.0 %collective-permute-start.11 = (bf16[1024,1280]{1,0:T(8,128)(2,1)}, bf16[1024,1280]{1,0:T(8,128)(2,1)}, u32[]{:S(2)}, u32[]{:S(2)}) collective-permute-start(bf16[1024,1280]{1,0:T(8,128)(2,1)} %broadcast_select_fusion.2), channel_id=1, source_target_pairs={{0,16},{16,0},{1,17},{17,1},{2,18},{18,2},{3,19},{19,3},{4,20},{20... | collective-permute-start | bytes 7864328 | tf_op jit(solution)/shard_map/ppermute | solution.py:28
  344.7 30.5 %all-to-all-start.2 = ((bf16[128,8,512]{0,2,1:T(8,128)(2,1)}), bf16[128,8,512]{0,2,1:T(8,128)(2,1)}, u32[]{:S(2)}, u32[]{:S(2)}) async-start(bf16[128,8,512]{0,2,1:T(8,128)(2,1)} %bitcast.45), calls=%async_computation.4 | async-start | bytes 2097152 | tf_op jit(solution)/shard_map/all_to_all | solution.py:33
  348.9 3.2 copy-start.4
  348.9 3.2 copy-start.6
  350.6 13.9 %collective-permute-start.9 = (bf16[512,512]{1,0:T(8,128)(2,1)S(1)}, bf16[512,512]{1,0:T(8,128)(2,1)S(1)}, u32[]{:S(2)}, u32[]{:S(2)}) collective-permute-start(bf16[512,512]{1,0:T(8,128)(2,1)S(1)} %add_convert_fusion.1), channel_id=1, source_target_pairs={{0,1},{1,0},{2,3},{3,2},{4,5},{5,4},{6,7},{7,6},{8,9},{9,8},{10,11... | collective-permute-start | bytes 1572872 | tf_op jit(solution)/shard_map/ppermute | solution.py:83
  364.7 2.0 collective-permute-start.10
  375.1 29.8 %all-to-all-start.1 = ((bf16[8,128,512]{1,2,0:T(8,128)(2,1)}), bf16[8,128,512]{1,2,0:T(8,128)(2,1)}, u32[]{:S(2)}, u32[]{:S(2)}) async-start(bf16[8,128,512]{1,2,0:T(8,128)(2,1)} %copy.16), calls=%async_computation.3 | async-start | bytes 2097152 | tf_op jit(solution)/shard_map/all_to_all | solution.py:93
  381.8 2.3 copy-start.9
  (1 other events, 0.7 us)
Sparse Core Ops, SparseCore 0:
  49.6 71.2 reduce-scatter.2
  123.7 53.5 all-gather.2
  207.9 69.5 reduce-scatter.4
  280.1 53.4 all-gather.4
where the time goes:
time: 414 us; the launch traced here: 413 us
  waiting for transfers between devices  288 us (70%)
  blocking collectives  33.8 us (8%)
  local copies, waits for them, and re-layouts  22.6 us (5%)
  starting transfers between devices  20.3 us (5%)
  matrix products  20 us (5%)
  between operations  14.7 us (4%)
  other arithmetic  14.5 us (4%)
    reduce_scatter x2, waiting for transfers between devices, body(): pre = lax.psum_scatter(part, 'dp', scatter_dimension=0, tiled=True)  117 us
    all_gather x2, waiting for transfers between devices, body(): hidden_all = lax.all_gather(hidden, 'dp', axis=0, tiled=True)  103 us
    ppermute x2, waiting for transfers between devices, body(): got = lax.ppermute(sent, 'tensor', [(0, 1), (1, 0)])  24.6 us
    unnamed x1, blocking collectives  19.5 us
    all_to_all x1, waiting for transfers between devices, body(): lax.all_to_all(state_own, 'dp', split_axis=0, concat_axis=1, tiled=True)  16.5 us
    ppermute x10, waiting for transfers between devices, swap(): return lax.ppermute(array, 'section', [(0, 1), (1, 0)])  11.3 us
    all_to_all x1, waiting for transfers between devices, body(): lax.all_to_all(tok_full, 'dp', split_axis=1, concat_axis=0, tiled=True)  11.2 us
    all_gather x1, blocking collectives, body(): tok_full = lax.all_gather(tok_half, 'tensor', axis=1, tiled=True)  9.97 us
  transfers between devices with their start and end apart: 19, of which 15 were waited for; matrix products, arithmetic and copies ran while one was open for 6% of the time, Pallas kernels for 0%

commit v1 on v0

--- a/solution.py
+++ b/solution.py
@@ -6,6 +6,22 @@
 EPS = 1e-06
 F32 = jnp.float32
 BF16 = jnp.bfloat16
+
+
+def exchange_in_pairs(x, axis, split, join):
+    ways, here = (lax.axis_size(axis), lax.axis_index(axis))
+    width = x.shape[split] // ways
+    lengths = list(x.shape)
+    lengths[split] = width
+    height = lengths[join]
+    lengths[join] = height * ways
+    full = jnp.zeros(lengths, x.dtype)
+    for mask in range(ways):
+        part = lax.dynamic_slice_in_dim(x, (here ^ mask) * width, width, axis=split)
+        if mask:
+            part = lax.ppermute(part, axis, [(d, d ^ mask) for d in range(ways)])
+        full = lax.dynamic_update_slice_in_dim(full, part, (here ^ mask) * height, axis=join)
+    return full
 
 
 def body(tokens, gain, w_up, w_down, cotangent):
@@ -90,7 +106,7 @@
         x = jnp.concatenate([new_a, new_b], axis=0)
         states.append(x)
     state_own = jnp.where(core == 0, states[0], states[1])
-    state_rows = lax.all_to_all(state_own, "dp", split_axis=0, concat_axis=1, tiled=True)
+    state_rows = exchange_in_pairs(state_own, "dp", 0, 1)
     state = lax.dynamic_slice_in_dim(state_rows, tensor_id * own_width, own_width, 1)
     hid_keep = jnp.where(core == 0, hiddens[0], hiddens[1])
     hid_got = swap(jnp.where(core == 0, hiddens[1], hiddens[0]))

time: 414 us -> 417 us (level)
  waiting for transfers between devices: 288 us -> 275 us
  starting transfers between devices: 20.3 us -> 28.7 us
  local copies, waits for them, and re-layouts: 22.6 us -> 27.8 us
    all_to_all x1 -> x0, waiting for transfers between devices: 16.5 us -> none  [body(): lax.all_to_all(state_own, 'dp', split_axis=0, concat_axis=1, tiled=True)]
    ppermute x0 -> x7, starting transfers between devices: none -> 12.9 us  [exchange_in_pairs(): part = lax.ppermute(part, axis, [(d, d ^ mask) for d in range(ways)])]
    ppermute x0 -> x7, waiting for transfers between devices: none -> 10.3 us  [exchange_in_pairs(): part = lax.ppermute(part, axis, [(d, d ^ mask) for d in range(ways)])]
    dynamic_update_slice x0 -> x7, local copies, waits for them, and re-layouts: none -> 6.63 us  [exchange_in_pairs(): lax.dynamic_update_slice_in_dim(full, part, (here ^ mask) * height, axis=...]
    all_to_all x1 -> x0, starting transfers between devices: 4.43 us -> none  [body(): lax.all_to_all(state_own, 'dp', split_axis=0, concat_axis=1, tiled=True)]
    unnamed x30 -> x38, local copies, waits for them, and re-layouts: 8.5 us -> 8.6 us
  transfers between devices with their start and end apart: 19 -> 25, of which waited for: 15 -> 17; matrix products, arithmetic and copies ran while one was open for 6% -> 7% of each run, Pallas kernels for 0% -> 0%
where the time goes in v1:
time: 417 us
  waiting for transfers between devices  275 us (66%)
  blocking collectives  33.8 us (8%)
  starting transfers between devices  28.7 us (7%)
  local copies, waits for them, and re-layouts  27.8 us (7%)
  matrix products  19.8 us (5%)
  other arithmetic  17.1 us (4%)
  between operations  14.7 us (4%)
    reduce_scatter x2, waiting for transfers between devices, body(): pre = lax.psum_scatter(part, 'dp', scatter_dimension=0, tiled=True)  117 us
    all_gather x2, waiting for transfers between devices, body(): hidden_all = lax.all_gather(hidden, 'dp', axis=0, tiled=True)  103 us
    ppermute x2, waiting for transfers between devices, body(): got = lax.ppermute(sent, 'tensor', [(0, 1), (1, 0)])  21.6 us
    unnamed x1, blocking collectives  19.5 us
    ppermute x7, starting transfers between devices, exchange_in_pairs(): part = lax.ppermute(part, axis, [(d, d ^ mask) for d in range(ways)])  12.9 us
    ppermute x10, waiting for transfers between devices, swap(): return lax.ppermute(array, 'section', [(0, 1), (1, 0)])  11.6 us
    all_to_all x1, waiting for transfers between devices, body(): lax.all_to_all(tok_full, 'dp', split_axis=1, concat_axis=0, tiled=True)  11.2 us
    ppermute x7, waiting for transfers between devices, exchange_in_pairs(): part = lax.ppermute(part, axis, [(d, d ^ mask) for d in range(ways)])  10.3 us
  transfers between devices with their start and end apart: 25, of which 17 were waited for; matrix products, arithmetic and copies ran while one was open for 7% of the time, Pallas kernels for 0%

profile of v1, /device:TPU:0, one launch (start us, length us, event | category | flops | bytes accessed | tf_op | source)
XLA Modules:
  0.0 416.6 jit_solution(8642460481807597480)
XLA Ops:
  8.2 10.0 %all_gather.12 = bf16[64,4096]{1,0:T(8,128)(2,1)S(1)} all-gather(bf16[64,2048]{1,0:T(8,128)(2,1)S(1)} %constant_dynamic-slice_fusion.8), channel_id=1, replica_groups=mesh['section'=2,'dp'=8,'tensor'=2] {'tensor'}, dimensions={1}, use_global_device_ids=true | all-gather | bytes 786432 | tf_op jit(solution)/shard_map/all_gather | solution.py:52
  19.0 6.2 %all-to-all-start = ((bf16[64,8,512]{2,0,1:T(8,128)(2,1)}), bf16[64,8,512]{2,0,1:T(8,128)(2,1)S(1)}, u32[]{:S(2)}, u32[]{:S(2)}) async-start(bf16[64,8,512]{2,0,1:T(8,128)(2,1)} %bitcast.40), calls=%async_computation | async-start | bytes 1048576 | tf_op jit(solution)/shard_map/all_to_all | solution.py:57
  25.3 2.5 dynamic-slice_bitcast_fusion.1
  27.7 11.2 %all-to-all-done = bf16[64,8,512]{2,0,1:T(8,128)(2,1)S(1)} async-done(((bf16[64,8,512]{2,0,1:T(8,128)(2,1)}), bf16[64,8,512]{2,0,1:T(8,128)(2,1)S(1)}, u32[]{:S(2)}, u32[]{:S(2)}) %all-to-all-start) | async-done | bytes 524320 | tf_op jit(solution)/shard_map/all_to_all | solution.py:57
  38.9 4.3 %all_gather.13 = bf16[1,4096]{1,0:T(2,128)(2,1)S(1)} all-gather(bf16[1,2048]{1,0:T(2,128)(2,1)S(1)} %copy-done.16), channel_id=1, replica_groups=mesh['section'=2,'dp'=8,'tensor'=2] {'tensor'}, dimensions={1}, use_global_device_ids=true | all-gather | bytes 12288 | tf_op jit(solution)/shard_map/all_gather | solution.py:66
  46.4 3.1 convolution_convert_fusion.1
  52.2 68.8 %reduce-scatter.3.cloned.1.call-done = bf16[128,1280]{1,0:T(8,128)(2,1)} async-done(((bf16[1024,1280]{1,0:T(8,128)(2,1)}), bf16[128,1280]{1,0:T(8,128)(2,1)}) %reduce-scatter.3.cloned.1.call-update) | async-done | bytes 327696 | tf_op jit(solution)/shard_map/reduce_scatter | solution.py:87
  120.9 2.0 fusion.30
  123.0 2.5 dynamic-slice_bitcast_fusion
  125.5 3.4 collective-permute-done.4
  128.9 48.4 %all-gather.3.cloned.1.call-done = bf16[1024,1280]{1,0:T(8,128)(2,1)} async-done(((bf16[128,1280]{1,0:T(8,128)(2,1)}), bf16[1024,1280]{1,0:T(8,128)(2,1)}) %all-gather.3.cloned.1.call-update) | async-done | bytes 2621456 | tf_op jit(solution)/shard_map/all_gather | solution.py:90
  177.3 3.7 fusion.10
  183.1 2.1 collective-permute-done.5
  188.2 12.5 %collective-permute-done.6 = bf16[512,512]{1,0:T(8,128)(2,1)S(1)} collective-permute-done((bf16[512,512]{1,0:T(8,128)(2,1)S(1)}, bf16[512,512]{1,0:T(8,128)(2,1)S(1)}, u32[]{:S(2)}, u32[]{:S(2)}) %collective-permute-start.6) | collective-permute-done | bytes 524320 | tf_op jit(solution)/shard_map/ppermute | solution.py:99
  203.0 4.8 %convolution_convert_fusion = bf16[1024,1280]{1,0:T(8,128)(2,1)} fusion(bf16[512,1280]{1,0:T(8,128)(2,1)} %collective-permute-done.2, pred[]{:T(512)S(6)} %eq.2, bf16[1,512,2560]{2,1,0:T(8,128)(2,1)S(1)} %copy-done.15, s32[]{:T(128)S(6)} %select_n.187, f32[512]{0:T(512)S(1)} %bitcast.47, bf16[512,512]{1,0:T(8,128)(2,1)S(1)} %get-tuple-element.15, ...), kind=kOutput, calls=%fused_computation.6 | convolution fusion | flops 1347289088 | bytes 6293509 | tf_op jit(solution)/shard_map/dot_general | solution.py:86
  209.9 19.5 %all-reduce = f32[1024]{0:T(1024)S(1)} all-reduce(f32[1024]{0:T(1024)S(1)} %multiply_reduce_fusion), channel_id=4, replica_groups=mesh['section'=2,'dp'=8,'tensor'=2] {'dp'}, use_global_device_ids=true, to_apply=%region_4.5.clone | all-reduce | flops 1024 | bytes 8192
  229.5 48.0 %reduce-scatter.5.cloned.1.call-done = bf16[128,1280]{1,0:T(8,128)(2,1)} async-done(((bf16[1024,1280]{1,0:T(8,128)(2,1)}), bf16[128,1280]{1,0:T(8,128)(2,1)}) %reduce-scatter.5.cloned.1.call-update) | async-done | bytes 327696 | tf_op jit(solution)/shard_map/reduce_scatter | solution.py:87
  279.5 54.1 %all-gather.5.cloned.1.call-done = bf16[1024,1280]{1,0:T(8,128)(2,1)} async-done(((bf16[128,1280]{1,0:T(8,128)(2,1)}), bf16[1024,1280]{1,0:T(8,128)(2,1)}) %all-gather.5.cloned.1.call-update) | async-done | bytes 2621456 | tf_op jit(solution)/shard_map/all_gather | solution.py:90
  333.6 4.0 fusion.11
  341.2 4.7 %all-to-all-start.1 = ((bf16[128,8,512]{0,2,1:T(8,128)(2,1)}), bf16[128,8,512]{0,2,1:T(8,128)(2,1)}, u32[]{:S(2)}, u32[]{:S(2)}) async-start(bf16[128,8,512]{0,2,1:T(8,128)(2,1)} %bitcast.42), calls=%async_computation.3 | async-start | bytes 2097152 | tf_op jit(solution)/shard_map/all_to_all | solution.py:49
  349.0 3.5 broadcast_select_fusion.2
  352.8 9.1 %collective-permute-done.9 = bf16[512,512]{1,0:T(8,128)(2,1)S(1)} collective-permute-done((bf16[512,512]{1,0:T(8,128)(2,1)S(1)}, bf16[512,512]{1,0:T(8,128)(2,1)S(1)}, u32[]{:S(2)}, u32[]{:S(2)}) %collective-permute-start.9) | collective-permute-done | bytes 524320 | tf_op jit(solution)/shard_map/ppermute | solution.py:99
  362.9 2.2 collective-permute-done.10
  372.4 2.3 copy.14
  374.7 2.3 collective-permute-start.17
  377.0 2.4 collective-permute-start.16
  381.0 2.9 collective-permute-start.14
  385.5 2.8 collective-permute-done.13
  388.3 2.5 collective-permute-start.15
  391.5 6.0 %collective-permute-done.14 = bf16[128,512]{1,0:T(8,128)(2,1)S(1)} collective-permute-done((bf16[128,512]{1,0:T(8,128)(2,1)}, bf16[128,512]{1,0:T(8,128)(2,1)S(1)}, u32[]{:S(2)}, u32[]{:S(2)}) %collective-permute-start.14) | collective-permute-done | bytes 131104 | tf_op jit(solution)/shard_map/ppermute | solution.py:22
  403.5 2.3 broadcast_select_fusion.1
  405.8 4.3 %fusion.7 = bf16[1,2560,512]{2,1,0:T(8,128)(2,1)} fusion(bf16[1024,512]{1,0:T(8,128)(2,1)S(1)} %bitcast.46, bf16[1024,1280]{1,0:T(8,128)(2,1)S(1)} %get-tuple-element.3, bf16[1024,1280]{1,0:T(8,128)(2,1)S(1)} %get-tuple-element.2), kind=kOutput, calls=%fused_computation.5 | convolution fusion | flops 2696151040 | bytes 8912896 | tf_op jit(solution)/shard_map/dot_general | solution.py:115
  (107 shorter events, 43.9 us)
Async XLA Ops:
  19.0 19.8 %copy-start.16 = (bf16[1,2048]{1,0:T(2,128)(2,1)S(1)}, bf16[1,2048]{1,0:T(2,128)(2,1)}, u32[]{:S(2)}) copy-start(bf16[1,2048]{1,0:T(2,128)(2,1)} %param.6) | copy-start | bytes 12292
  19.0 19.8 %all-to-all-start = ((bf16[64,8,512]{2,0,1:T(8,128)(2,1)}), bf16[64,8,512]{2,0,1:T(8,128)(2,1)S(1)}, u32[]{:S(2)}, u32[]{:S(2)}) async-start(bf16[64,8,512]{2,0,1:T(8,128)(2,1)} %bitcast.40), calls=%async_computation | async-start | bytes 1048576 | tf_op jit(solution)/shard_map/all_to_all | solution.py:57
  25.2 95.7 %reduce-scatter.3.cloned.1.call-start = ((), (), s32[]{:S(2)}) async-start(), calls=%async_computation.4 | async-start | bytes 2949120 | tf_op jit(solution)/shard_map/reduce_scatter | solution.py:87
  27.7 17.3 %collective-permute-start.2 = (bf16[512,1280]{1,0:T(8,128)(2,1)}, bf16[512,1280]{1,0:T(8,128)(2,1)}, u32[]{:S(2)}, u32[]{:S(2)}) collective-permute-start(bf16[512,1280]{1,0:T(8,128)(2,1)} %dynamic-slice_bitcast_fusion.1), channel_id=1, source_target_pairs={{0,16},{16,0},{1,17},{17,1},{2,18},{18,2},{3,19},{19,3},{4,20},{20... | collective-permute-start | bytes 3932168 | tf_op jit(solution)/shard_map/ppermute | solution.py:44
  38.9 5.6 %collective-permute-start = (bf16[512,512]{1,0:T(8,128)(2,1)S(1)}, bf16[512,512]{1,0:T(8,128)(2,1)S(1)}, u32[]{:S(2)}, u32[]{:S(2)}) collective-permute-start(bf16[512,512]{1,0:T(8,128)(2,1)S(1)} %bitcast.43), channel_id=1, source_target_pairs={{0,16},{16,0},{1,17},{17,1},{2,18},{18,2},{3,19},{19,3},{4,20},{20... | collective-permute-start | bytes 1572872 | tf_op jit(solution)/shard_map/ppermute | solution.py:44
  43.2 1.2 collective-permute-start.1
  49.5 127.8 %all-gather.3.cloned.1.call-start = ((), (), s32[]{:S(2)}) async-start(), calls=%async_computation.5 | async-start | bytes 2949120 | tf_op jit(solution)/shard_map/all_gather | solution.py:90
  49.7 2.3 collective-permute-start.3
  123.0 154.5 %reduce-scatter.5.cloned.1.call-start = ((), (), s32[]{:S(2)}) async-start(), calls=%async_computation.6 | async-start | bytes 2949120 | tf_op jit(solution)/shard_map/reduce_scatter | solution.py:87
  125.5 3.4 collective-permute-start.4
  183.1 2.1 collective-permute-start.5
  186.6 16.3 %copy-start.15 = (bf16[1,512,2560]{2,1,0:T(8,128)(2,1)S(1)}, bf16[1,512,2560]{2,1,0:T(8,128)(2,1)}, u32[]{:S(2)}) copy-start(bf16[1,512,2560]{2,1,0:T(8,128)(2,1)} %param.7) | copy-start | bytes 7864324
  186.7 14.0 %collective-permute-start.6 = (bf16[512,512]{1,0:T(8,128)(2,1)S(1)}, bf16[512,512]{1,0:T(8,128)(2,1)S(1)}, u32[]{:S(2)}, u32[]{:S(2)}) collective-permute-start(bf16[512,512]{1,0:T(8,128)(2,1)S(1)} %add_convert_fusion.3), channel_id=1, source_target_pairs={{0,1},{1,0},{2,3},{3,2},{4,5},{5,4},{6,7},{7,6},{8,9},{9,8},{10,11... | collective-permute-start | bytes 1572872 | tf_op jit(solution)/shard_map/ppermute | solution.py:99
  200.9 2.0 collective-permute-start.7
  203.0 6.7 %copy-start.3 = (bf16[512,512]{1,0:T(8,128)(2,1)}, bf16[512,512]{1,0:T(8,128)(2,1)S(1)}, u32[]{:S(2)}) copy-start(bf16[512,512]{1,0:T(8,128)(2,1)S(1)} %get-tuple-element.14) | copy-start | bytes 1572868
  203.0 6.7 %copy-start.6 = (bf16[512,512]{1,0:T(8,128)(2,1)}, bf16[512,512]{1,0:T(8,128)(2,1)S(1)}, u32[]{:S(2)}) copy-start(bf16[512,512]{1,0:T(8,128)(2,1)S(1)} %get-tuple-element.15) | copy-start | bytes 1572868
  207.8 125.9 %all-gather.5.cloned.1.call-start = ((), (), s32[]{:S(2)}) async-start(), calls=%async_computation.7 | async-start | bytes 2949120 | tf_op jit(solution)/shard_map/all_gather | solution.py:90
  279.5 60.4 %copy-start.12 = (bf16[1,128,4096]{2,1,0:T(8,128)(2,1)S(1)}, bf16[1,128,4096]{2,1,0:T(8,128)(2,1)}, u32[]{:S(2)}) copy-start(bf16[1,128,4096]{2,1,0:T(8,128)(2,1)} %param.9) | copy-start | bytes 3145732
  339.9 6.0 %collective-permute-start.8 = (bf16[512,512]{1,0:T(8,128)(2,1)}, bf16[512,512]{1,0:T(8,128)(2,1)}, u32[]{:S(2)}, u32[]{:S(2)}) collective-permute-start(bf16[512,512]{1,0:T(8,128)(2,1)} %dynamic-slice_convert_fusion), channel_id=1, source_target_pairs={{0,16},{16,0},{1,17},{17,1},{2,18},{18,2},{3,19},{19,3},{4,20},{20... | collective-permute-start | bytes 1572872 | tf_op jit(solution)/shard_map/ppermute | solution.py:44
  341.2 7.8 %copy-start.1 = (bf16[1024,1280]{1,0:T(8,128)(2,1)S(1)}, bf16[1024,1280]{1,0:T(8,128)(2,1)}, u32[]{:S(2)}) copy-start(bf16[1024,1280]{1,0:T(8,128)(2,1)} %all-gather.3.cloned.1.call-done) | copy-start | bytes 7864324
  341.2 31.2 %all-to-all-start.1 = ((bf16[128,8,512]{0,2,1:T(8,128)(2,1)}), bf16[128,8,512]{0,2,1:T(8,128)(2,1)}, u32[]{:S(2)}, u32[]{:S(2)}) async-start(bf16[128,8,512]{0,2,1:T(8,128)(2,1)} %bitcast.42), calls=%async_computation.3 | async-start | bytes 2097152 | tf_op jit(solution)/shard_map/all_to_all | solution.py:49
  347.5 14.4 %collective-permute-start.9 = (bf16[512,512]{1,0:T(8,128)(2,1)S(1)}, bf16[512,512]{1,0:T(8,128)(2,1)S(1)}, u32[]{:S(2)}, u32[]{:S(2)}) collective-permute-start(bf16[512,512]{1,0:T(8,128)(2,1)S(1)} %add_convert_fusion.1), channel_id=1, source_target_pairs={{0,1},{1,0},{2,3},{3,2},{4,5},{5,4},{6,7},{7,6},{8,9},{9,8},{10,11... | collective-permute-start | bytes 1572872 | tf_op jit(solution)/shard_map/ppermute | solution.py:99
  352.5 51.0 %collective-permute-start.18 = (bf16[1024,1280]{1,0:T(8,128)(2,1)}, bf16[1024,1280]{1,0:T(8,128)(2,1)}, u32[]{:S(2)}, u32[]{:S(2)}) collective-permute-start(bf16[1024,1280]{1,0:T(8,128)(2,1)} %broadcast_select_fusion.2), channel_id=1, source_target_pairs={{0,16},{16,0},{1,17},{17,1},{2,18},{18,2},{3,19},{19,3},{4,20},{20... | collective-permute-start | bytes 7864328 | tf_op jit(solution)/shard_map/ppermute | solution.py:44
  362.9 2.3 collective-permute-start.10
  368.7 10.7 %collective-permute-start.11 = (bf16[128,512]{1,0:T(8,128)(2,1)}, bf16[128,512]{1,0:T(8,128)(2,1)}, u32[]{:S(2)}, u32[]{:S(2)}) collective-permute-start(bf16[128,512]{1,0:T(8,128)(2,1)} %get-tuple-element.10), channel_id=1, source_target_pairs={{0,2},{2,0},{4,6},{6,4},{8,10},{10,8},{12,14},{14,12},{1,3},{3,1},... | collective-permute-start | bytes 393224 | tf_op jit(solution)/shard_map/ppermute | solution.py:22
  370.2 10.8 %collective-permute-start.12 = (bf16[128,512]{1,0:T(8,128)(2,1)}, bf16[128,512]{1,0:T(8,128)(2,1)}, u32[]{:S(2)}, u32[]{:S(2)}) collective-permute-start(bf16[128,512]{1,0:T(8,128)(2,1)} %get-tuple-element.9), channel_id=1, source_target_pairs={{0,4},{2,6},{4,0},{6,2},{8,12},{10,14},{12,8},{14,10},{1,5},{3,7},... | collective-permute-start | bytes 393224 | tf_op jit(solution)/shard_map/ppermute | solution.py:22
  374.7 28.9 %copy-start.2 = (bf16[1024,1280]{1,0:T(8,128)(2,1)S(1)}, bf16[1024,1280]{1,0:T(8,128)(2,1)}, u32[]{:S(2)}) copy-start(bf16[1024,1280]{1,0:T(8,128)(2,1)} %all-gather.5.cloned.1.call-done) | copy-start | bytes 7864324
  374.7 26.3 %collective-permute-start.17 = (bf16[128,512]{1,0:T(8,128)(2,1)S(1)}, bf16[128,512]{1,0:T(8,128)(2,1)S(1)}, u32[]{:S(2)}, u32[]{:S(2)}) collective-permute-start(bf16[128,512]{1,0:T(8,128)(2,1)S(1)} %get-tuple-element.4), channel_id=1, source_target_pairs={{0,14},{2,12},{4,10},{6,8},{8,6},{10,4},{12,2},{14,0},{1,15},{3,13... | collective-permute-start | bytes 393224 | tf_op jit(solution)/shard_map/ppermute | solution.py:22
  377.0 23.3 %collective-permute-start.16 = (bf16[128,512]{1,0:T(8,128)(2,1)S(1)}, bf16[128,512]{1,0:T(8,128)(2,1)S(1)}, u32[]{:S(2)}, u32[]{:S(2)}) collective-permute-start(bf16[128,512]{1,0:T(8,128)(2,1)S(1)} %get-tuple-element.5), channel_id=1, source_target_pairs={{0,12},{2,14},{4,8},{6,10},{8,4},{10,6},{12,0},{14,2},{1,13},{3,15... | collective-permute-start | bytes 393224 | tf_op jit(solution)/shard_map/ppermute | solution.py:22
  379.4 8.9 %collective-permute-start.13 = (bf16[128,512]{1,0:T(8,128)(2,1)}, bf16[128,512]{1,0:T(8,128)(2,1)S(1)}, u32[]{:S(2)}, u32[]{:S(2)}) collective-permute-start(bf16[128,512]{1,0:T(8,128)(2,1)} %get-tuple-element.8), channel_id=1, source_target_pairs={{0,6},{2,4},{4,2},{6,0},{8,14},{10,12},{12,10},{14,8},{1,7},{3,5},... | collective-permute-start | bytes 393224 | tf_op jit(solution)/shard_map/ppermute | solution.py:22
  381.0 16.5 %collective-permute-start.14 = (bf16[128,512]{1,0:T(8,128)(2,1)}, bf16[128,512]{1,0:T(8,128)(2,1)S(1)}, u32[]{:S(2)}, u32[]{:S(2)}) collective-permute-start(bf16[128,512]{1,0:T(8,128)(2,1)} %get-tuple-element.7), channel_id=1, source_target_pairs={{0,8},{2,10},{4,12},{6,14},{8,0},{10,2},{12,4},{14,6},{1,9},{3,11}... | collective-permute-start | bytes 393224 | tf_op jit(solution)/shard_map/ppermute | solution.py:22
  388.3 11.3 %collective-permute-start.15 = (bf16[128,512]{1,0:T(8,128)(2,1)S(1)}, bf16[128,512]{1,0:T(8,128)(2,1)S(1)}, u32[]{:S(2)}, u32[]{:S(2)}) collective-permute-start(bf16[128,512]{1,0:T(8,128)(2,1)S(1)} %get-tuple-element.6), channel_id=1, source_target_pairs={{0,10},{2,8},{4,14},{6,12},{8,2},{10,0},{12,6},{14,4},{1,11},{3,9}... | collective-permute-start | bytes 393224 | tf_op jit(solution)/shard_map/ppermute | solution.py:22
  (11 other events, 26.6 us)
Sparse Core Ops, SparseCore 0:
  49.6 71.2 reduce-scatter.2
  123.7 53.5 all-gather.2
  207.9 69.5 reduce-scatter.4
  280.1 53.4 all-gather.4
